TPU v7x, 32 devices: a 4x2x2 block of a 4x4x8 slice. The times are simulated.
32 devices in a mesh: dp: 4 (over y, z), tp: 8 (over x, core).
Axes of the slice: x: 4, y: 2, z: 2, core: 2. Of those that a mesh axis runs over, the one named last changes fastest.
The devices are a block of a 4x4x8 slice.
Arguments:
- x_in: bfloat16 [8, 64, 4096], P('dp'), parts along dimension 0
- start_pos: int32 [8], P('dp'), parts along dimension 0
- kv_state: float32 [8, 16, 256, 512], P('dp', 'tp'), parts along dimension 0
- ln1_gain: float32 [4096], replicated
- ln1_bias: float32 [4096], replicated
- w_q: bfloat16 [4096, 4096], P(None, 'tp')
- w_k: bfloat16 [4096, 4096], P(None, 'tp')
- w_v: bfloat16 [4096, 8192], P(None, 'tp')
- w_g: bfloat16 [4096, 8192], P(None, 'tp')
- w_o: bfloat16 [8192, 4096], P('tp')
- ln2_gain: float32 [4096], replicated
- ln2_bias: float32 [4096], replicated
- w_up: bfloat16 [4096, 8192], P(None, 'tp')
- w_down: bfloat16 [8192, 4096], P('tp')
Outputs:
- output 1: bfloat16 [8, 64, 4096], P('dp'), parts along dimension 0
- output 2: float32 [8, 16, 256, 512], P('dp', 'tp'), parts along dimension 0
There are 4 independent parts. A program takes and returns all parts, laid end to end along the dimension named above; an argument that names none is the same for every part.
All inputs are finite; a program needn't handle non-finite values.
Results may differ from a plain program's by a relative error of at most 0.0145638.
Values are sent between devices in bfloat16 or wider.
A program may use at most 768 MiB of HBM per device.

v0:
```python
import jax
import jax.numpy as jnp
from jax import lax
from jax.sharding import PartitionSpec as P

NORM_EPS = 1e-5
GROUP_EPS = 1e-6
ROPE_BASE = 10000.0


def layer_norm(x_f32, norm_gain, norm_bias):
    row_mean = jnp.mean(x_f32, axis=-1, keepdims=True)
    centered = x_f32 - row_mean
    variance = jnp.mean(centered * centered, axis=-1, keepdims=True)
    return centered * lax.rsqrt(variance + NORM_EPS) * norm_gain + norm_bias


def rotate_half(head_vecs, cos_t, sin_t):
    half_dim = head_vecs.shape[-1] // 2
    first_half = head_vecs[..., :half_dim]
    second_half = head_vecs[..., half_dim:]
    return jnp.concatenate([first_half * cos_t - second_half * sin_t, second_half * cos_t + first_half * sin_t], axis=-1)


def rope_tables(first_pos, chunk_len, key_dim):
    half_dim = key_dim // 2
    inv_freq = jnp.power(ROPE_BASE, -jnp.arange(half_dim).astype(jnp.float32) / half_dim)
    positions = (first_pos[:, None] + jnp.arange(chunk_len)[None, :]).astype(jnp.float32)
    angles = positions[:, :, None] * inv_freq
    return jnp.cos(angles)[:, :, None, :], jnp.sin(angles)[:, :, None, :]


def head_log_decay(head_ids):
    return jnp.log1p(-jnp.exp2(-5.0 - head_ids.astype(jnp.float32)))


def project_heads(h_one, cos_t, sin_t, w_q, w_k, w_v, w_g, num_heads):
    d_model = h_one.shape[-1]
    key_dim = w_q.shape[1] // num_heads
    val_dim = w_v.shape[1] // num_heads
    q_raw = jnp.einsum('bcd,dhk->bchk', h_one, w_q.reshape(d_model, num_heads, key_dim), preferred_element_type=jnp.float32)
    k_raw = jnp.einsum('bcd,dhk->bchk', h_one, w_k.reshape(d_model, num_heads, key_dim), preferred_element_type=jnp.float32)
    queries = rotate_half(q_raw, cos_t, sin_t).astype(jnp.bfloat16)
    keys = (rotate_half(k_raw, cos_t, sin_t) * key_dim ** -0.5).astype(jnp.bfloat16)
    values = jnp.einsum('bcd,dhe->bche', h_one, w_v.reshape(d_model, num_heads, val_dim), preferred_element_type=jnp.float32).astype(jnp.bfloat16)
    gates = jnp.einsum('bcd,dhe->bche', h_one, w_g.reshape(d_model, num_heads, val_dim), preferred_element_type=jnp.float32)
    return queries, keys, values, gates


def mix_heads(queries, keys, values_f32, gates, state_in, log_gamma, w_o):
    chunk_len = queries.shape[1]
    num_heads = queries.shape[2]
    val_dim = values_f32.shape[3]
    step_ids = jnp.arange(chunk_len)
    step_gap = step_ids[:, None] - step_ids[None, :]
    inner_decay = jnp.where(step_gap[None] >= 0, jnp.exp(jnp.maximum(step_gap, 0).astype(jnp.float32)[None] * log_gamma[:, None, None]), 0.0)
    query_decay = jnp.exp((step_ids + 1).astype(jnp.float32)[:, None] * log_gamma[None, :])
    scores = jnp.einsum('bchk,bjhk->bhcj', queries, keys, preferred_element_type=jnp.float32) * inner_decay
    retained = jnp.einsum('bhcj,bjhe->bche', scores, values_f32) + jnp.einsum('bchk,bhke->bche', queries.astype(jnp.float32), state_in) * query_decay[:, :, None]
    row_mean = jnp.mean(retained, axis=-1, keepdims=True)
    centered = retained - row_mean
    variance = jnp.mean(centered * centered, axis=-1, keepdims=True)
    normed = centered * lax.rsqrt(variance + GROUP_EPS)
    mixed = (jax.nn.silu(gates) * normed).astype(jnp.bfloat16)
    return jnp.einsum('bche,hed->bcd', mixed, w_o.reshape(num_heads, val_dim, w_o.shape[1]), preferred_element_type=jnp.float32)


def chunk_state(keys, values_f32, log_gamma):
    chunk_len = keys.shape[1]
    step_ids = jnp.arange(chunk_len)
    key_decay = jnp.exp((chunk_len - 1 - step_ids).astype(jnp.float32)[:, None] * log_gamma[None, :])
    return jnp.einsum('bjhk,bjhe->bhke', keys.astype(jnp.float32) * key_decay[:, :, None], values_f32)


def feed_forward(x_mid, ln2_gain, ln2_bias, w_up, w_down):
    h_two = layer_norm(x_mid.astype(jnp.float32), ln2_gain, ln2_bias).astype(jnp.bfloat16)
    activated = jax.nn.gelu(jnp.einsum('bcd,df->bcf', h_two, w_up, preferred_element_type=jnp.float32), approximate=False).astype(jnp.bfloat16)
    return jnp.einsum('bcf,fd->bcd', activated, w_down, preferred_element_type=jnp.float32)


def solution(mesh):
    def local_layer(x_in, start_pos, kv_state, ln1_gain, ln1_bias, w_q, w_k, w_v, w_g, w_o, ln2_gain, ln2_bias, w_up, w_down):
        local_heads = kv_state.shape[1]
        chunk_len = x_in.shape[1]
        head_ids = lax.axis_index('tp') * local_heads + jnp.arange(local_heads)
        log_gamma = head_log_decay(head_ids)
        x_f32 = x_in.astype(jnp.float32)
        h_one = layer_norm(x_f32, ln1_gain, ln1_bias).astype(jnp.bfloat16)
        cos_t, sin_t = rope_tables(start_pos, chunk_len, kv_state.shape[2])
        queries, keys, values, gates = project_heads(h_one, cos_t, sin_t, w_q, w_k, w_v, w_g, local_heads)
        values_f32 = values.astype(jnp.float32)
        attn_part = mix_heads(queries, keys, values_f32, gates, kv_state, log_gamma, w_o).astype(jnp.bfloat16)
        new_state = jnp.exp(chunk_len * log_gamma)[:, None, None] * kv_state + chunk_state(keys, values_f32, log_gamma)
        attn_out = lax.psum(attn_part, 'tp')
        x_mid = (x_f32 + attn_out.astype(jnp.float32)).astype(jnp.bfloat16)
        ffn_part = feed_forward(x_mid, ln2_gain, ln2_bias, w_up, w_down).astype(jnp.bfloat16)
        ffn_out = lax.psum(ffn_part, 'tp')
        x_out = (x_mid.astype(jnp.float32) + ffn_out.astype(jnp.float32)).astype(jnp.bfloat16)
        return x_out, new_state

    in_specs = (P('dp', None, None), P('dp'), P('dp', 'tp', None, None), P(), P(), P(None, 'tp'), P(None, 'tp'), P(None, 'tp'), P(None, 'tp'), P('tp', None), P(), P(), P(None, 'tp'), P('tp', None))
    out_specs = (P('dp', None, None), P('dp', 'tp', None, None))
    return jax.shard_map(local_layer, mesh=mesh, in_specs=in_specs, out_specs=out_specs, check_vma=False)
```

profile of v0, /device:TPU:81, one launch (start us, length us, event | category | flops | bytes accessed | tf_op | source)
XLA Modules:
  0.0 164.7 jit_solution(9171510052861706363)
XLA Ops:
  7.2 0.0 copy-start
  7.2 0.0 copy-start.6
  7.2 0.0 copy-start.7
  7.2 0.1 all-reduce.3.cloned.1.call-start
  7.4 0.8 add_convert_fusion.1
  8.2 1.5 convert_reduce_fusion.1
  9.7 1.7 %fusion.24 = f32[2,64]{1,0:T(2,128)S(1)} fusion(bf16[2,64,4096]{2,1,0:T(8,128)(2,1)} %param.14, f32[2,64]{1,0:T(2,128)S(1)} %broadcast_multiply_fusion.2), kind=kLoop, calls=%fused_computation.33 | loop fusion | flops 2097024 | bytes 1049600 | tf_op jit(solution)/shard_map/reduce_sum | solution.py:14
  11.3 0.0 copy-done
  11.3 0.0 copy-done.6
  11.3 0.0 copy-done.7
  11.3 0.0 copy-start.4
  11.3 4.9 %fusion.32 = bf16[2,64,2,512]{3,1,2,0:T(8,128)(2,1)S(1)} fusion(bf16[512,2,8,512]{3,2,1,0:T(8,128)(2,1)} %bitcast.80, bf16[2,64,4096]{2,1,0:T(8,128)(2,1)S(1)} %copy-done, f32[4096]{0:T(1024)S(1)} %copy-done.6, f32[4096]{0:T(1024)S(1)} %copy-done.7, f32[2,64]{1,0:T(2,128)S(1)} %add_rsqrt_fusion.2, f32[2,64]{1,0:T(2,128)S(1)} %broadcast_multiply_fusion.2), kind=kOutput, calls=%fused_computation.44 | convolution fusion | flops 1077018624 | bytes 9733120 | tf_op jit(solution)/shard_map/bcd,dhe->bche/dot_general | solution.py:45
  16.2 0.0 copy-start.3
  16.2 0.0 copy-done.4
  16.2 0.0 copy-start.5
  16.2 0.8 fusion.14
  17.1 1.4 copy-done.5
  18.5 0.8 fusion.12
  19.3 0.1 multiply_exponential_fusion
  19.3 0.1 exponential_select_fusion
  19.4 0.3 multiply_cosine_fusion
  19.8 0.1 multiply_subtract_fusion
  19.8 0.3 copy-done.1
  20.1 0.3 fusion.30
  20.4 0.0 copy-done.3
  20.4 0.4 fusion.140
  20.8 0.2 multiply_reduce_fusion
  21.1 9.3 %fusion.8 = bf16[2,64,4096]{2,1,0:T(8,128)(2,1)} fusion(bf16[2,512,4096,1]{2,1,0,3:T(8,128)(2,1)} %bitcast.81, bf16[512,2,8,512]{3,2,1,0:T(8,128)(2,1)} %bitcast.82, f32[2,64,2,512]{3,1,2,0:T(8,128)S(1)} %get-tuple-element.17, f32[2,64,2]{1,2,0:T(2,128)S(1)} %add_rsqrt_fusion, f32[2,64,2]{1,2,0:T(2,128)S(1)} %broadcast_multiply_fusion, ...), kind=kOutput, calls=%fused_computation.11 | convolution fusion | flops 2152202240 | bytes 19434496 | tf_op jit(solution)/shard_map/bche,hed->bcd/dot_general | solution.py:65
  30.4 0.1 all-reduce.3.cloned.1.call-update
  30.4 0.0 copy-start.8
  30.5 0.0 copy-start.9
  30.5 0.2 all-reduce.5.cloned.1.call-start
  30.7 58.2 %all-reduce.3.cloned.1.call-done = bf16[2,64,4096]{2,1,0:T(8,128)(2,1)} async-done(((bf16[2,64,4096]{2,1,0:T(8,128)(2,1)}), bf16[2,64,4096]{2,1,0:T(8,128)(2,1)}) %all-reduce.3.cloned.1.call-update) | async-done | bytes 1048592 | tf_op jit(solution)/shard_map/psum | solution.py:94
  89.0 1.8 %convert_reduce_fusion = (f32[2,64]{1,0:T(2,128)S(1)}, bf16[2,64,4096]{2,1,0:T(8,128)(2,1)S(1)}) fusion(bf16[2,64,4096]{2,1,0:T(8,128)(2,1)} %all-reduce.3.cloned.1.call-done, bf16[2,64,4096]{2,1,0:T(8,128)(2,1)S(1)} %copy-done), kind=kLoop, calls=%fused_computation.21 | loop fusion | flops 3145600 | bytes 3146240 | tf_op jit(solution)/shard_map/reduce_sum | solution.py:12
  90.7 0.4 fusion.20
  91.2 0.0 copy-done.8
  91.2 0.0 copy-done.9
  91.2 0.0 slice-start.1
  91.2 5.0 %fusion.85 = (u8[64,1024]{1,0:T(8,128)(4,1)S(1)}, u8[64,1024]{1,0:T(8,128)(4,1)S(1)}, f32[2,64,1024]{2,1,0:T(8,128)S(1)}) fusion(bf16[4096,1024]{1,0:T(8,128)(2,1)} %param.26, bf16[2,64,4096]{2,1,0:T(8,128)(2,1)S(1)} %get-tuple-element.5, f32[4096]{0:T(1024)S(1)} %copy-done.8, f32[4096]{0:T(1024)S(1)} %copy-done.9, f32[2,64]{1,0:T(2,128)S(1)} %add_rsqrt_fusion.1, ...), kind=kOutput, calls=%fused_computation.117 | convolution fusion | flops 1078460416 | bytes 10126336 | tf_op jit(solution)/shard_map/bcd,df->bcf/dot_general | solution.py:77
  96.2 0.0 slice-done
  96.3 0.0 slice-done.1
  96.3 0.0 copy-start.2
  96.3 3.4 %fusion.9 = bf16[2,64,4096]{2,1,0:T(8,128)(2,1)} fusion(bf16[1024,4096]{1,0:T(8,128)(2,1)S(1)} %bitcast.84, f32[2,64,1024]{2,1,0:T(8,128)S(1)} %get-tuple-element.18, u8[64,1024]{1,0:T(8,128)(4,1)S(1)} %get-tuple-element.3, u8[64,1024]{1,0:T(8,128)(4,1)S(1)} %get-tuple-element.2), kind=kOutput, calls=%fused_computation.12 | convolution fusion | flops 1083441152 | bytes 10092544 | tf_op jit(solution)/shard_map/bcf,fd->bcd/dot_general | solution.py:78
  99.7 0.1 all-reduce.5.cloned.1.call-update
  99.7 0.0 copy-done.2
  99.7 2.8 %multiply_add_fusion = f32[2,2,256,512]{3,2,1,0:T(8,128)} fusion(f32[2,2,256,512]{3,2,1,0:T(8,128)S(1)} %copy-done.2, bf16[2,64,2,512]{3,1,2,0:T(8,128)(2,1)} %copy-done.3, f32[2]{0:T(128)S(1)} %multiply_exponential_fusion.2, f32[64,2]{0,1:T(2,128)S(1)} %get-tuple-element.14, f32[2,64,2,128]{3,1,2,0:T(8,128)S(1)} %get-tuple-element.7, ...), kind=kOutput, calls=%fused_computation.39 | convolution fusion | flops 68485120 | bytes 4719112 | tf_op jit(solution)/shard_map/bjhk,bjhe->bhke/dot_general | solution.py:72
  102.6 52.8 %all-reduce.5.cloned.1.call-done = bf16[2,64,4096]{2,1,0:T(8,128)(2,1)} async-done(((bf16[2,64,4096]{2,1,0:T(8,128)(2,1)}), bf16[2,64,4096]{2,1,0:T(8,128)(2,1)}) %all-reduce.5.cloned.1.call-update) | async-done | bytes 1048592 | tf_op jit(solution)/shard_map/psum | solution.py:97
  155.4 2.4 %fusion.29 = bf16[2,64,4096]{2,1,0:T(8,128)(2,1)} fusion(bf16[2,64,4096]{2,1,0:T(8,128)(2,1)S(1)} %get-tuple-element.5, bf16[2,64,4096]{2,1,0:T(8,128)(2,1)} %all-reduce.5.cloned.1.call-done), kind=kLoop, calls=%fused_computation.38 | loop fusion | flops 2097152 | bytes 3145728 | tf_op jit(solution)/shard_map/convert_element_type | solution.py:98
  (15 shorter events, 0.1 us)
Async XLA Ops:
  7.2 4.1 %copy-start = (bf16[2,64,4096]{2,1,0:T(8,128)(2,1)S(1)}, bf16[2,64,4096]{2,1,0:T(8,128)(2,1)}, u32[]{:S(2)}) copy-start(bf16[2,64,4096]{2,1,0:T(8,128)(2,1)} %param.14) | copy-start | bytes 3145732
  7.2 4.1 %copy-start.6 = (f32[4096]{0:T(1024)S(1)}, f32[4096]{0:T(1024)}, u32[]{:S(2)}) copy-start(f32[4096]{0:T(1024)} %param.18) | copy-start | bytes 49156
  7.2 4.1 %copy-start.7 = (f32[4096]{0:T(1024)S(1)}, f32[4096]{0:T(1024)}, u32[]{:S(2)}) copy-start(f32[4096]{0:T(1024)} %param.17) | copy-start | bytes 49156
  7.2 81.7 %all-reduce.3.cloned.1.call-start = ((), (), s32[]{:S(2)}) async-start(), calls=%async_computation | async-start | bytes 2097152 | tf_op jit(solution)/shard_map/psum | solution.py:94
  11.3 4.9 %copy-start.4 = (bf16[4096,512]{1,0:T(8,128)(2,1)S(1)}, bf16[4096,512]{1,0:T(8,128)(2,1)}, u32[]{:S(2)}) copy-start(bf16[4096,512]{1,0:T(8,128)(2,1)} %param.19) | copy-start | bytes 12582916
  16.2 4.2 %copy-start.3 = (bf16[2,64,2,512]{3,1,2,0:T(8,128)(2,1)}, bf16[2,64,2,512]{3,1,2,0:T(8,128)(2,1)S(1)}, u32[]{:S(2)}) copy-start(bf16[2,64,2,512]{3,1,2,0:T(8,128)(2,1)S(1)} %fusion.32) | copy-start | bytes 786436
  16.2 2.3 %copy-start.5 = (bf16[4096,512]{1,0:T(8,128)(2,1)S(1)}, bf16[4096,512]{1,0:T(8,128)(2,1)}, u32[]{:S(2)}) copy-start(bf16[4096,512]{1,0:T(8,128)(2,1)} %param.20) | copy-start | bytes 12582916
  18.5 1.6 copy-start.1
  30.4 60.7 %copy-start.8 = (f32[4096]{0:T(1024)S(1)}, f32[4096]{0:T(1024)}, u32[]{:S(2)}) copy-start(f32[4096]{0:T(1024)} %param.25) | copy-start | bytes 49156
  30.5 60.7 %copy-start.9 = (f32[4096]{0:T(1024)S(1)}, f32[4096]{0:T(1024)}, u32[]{:S(2)}) copy-start(f32[4096]{0:T(1024)} %param.24) | copy-start | bytes 49156
  30.5 125.0 %all-reduce.5.cloned.1.call-start = ((), (), s32[]{:S(2)}) async-start(), calls=%async_computation.1 | async-start | bytes 2097152 | tf_op jit(solution)/shard_map/psum | solution.py:97
  88.9 7.3 %slice-start = ((s8[8388608]{0:T(1024)(128)(4,1)}), s8[4194304]{0:T(1024)(128)(4,1)S(1)}, s32[]{:S(2)}) async-start(s8[8388608]{0:T(1024)(128)(4,1)} %bitcast.83), calls=%async_computation.2 | async-start | bytes 8388608
  91.2 5.1 %slice-start.1 = ((s8[8388608]{0:T(1024)(128)(4,1)}), s8[4194304]{0:T(1024)(128)(4,1)S(1)}, s32[]{:S(2)}) async-start(s8[8388608]{0:T(1024)(128)(4,1)} %bitcast.83), calls=%async_computation.3 | async-start | bytes 8388608
  96.3 3.5 %copy-start.2 = (f32[2,2,256,512]{3,2,1,0:T(8,128)S(1)}, f32[2,2,256,512]{3,2,1,0:T(8,128)}, u32[]{:S(2)}) copy-start(f32[2,2,256,512]{3,2,1,0:T(8,128)} %param.16) | copy-start | bytes 6291460
Sparse Core Ops, SparseCore 0:
  30.6 58.3 all-reduce.2
  99.8 55.5 all-reduce.4
where the time goes:
time: 166 us; the launch traced here: 165 us
  waiting for transfers between devices  111 us (67%)
  matrix products  27.7 us (17%)
  between operations  14.3 us (9%)
  other arithmetic  9.44 us (6%)
  local copies, waits for them, and re-layouts  1.77 us (1%)
    psum x1, waiting for transfers between devices, local_layer(): attn_out = lax.psum(attn_part, 'tp')  58.2 us
    psum x1, waiting for transfers between devices, local_layer(): ffn_out = lax.psum(ffn_part, 'tp')  52.8 us
    dot_general x1, matrix products, mix_heads(): jnp.einsum('bche,hed->bcd', mixed, w_o.reshape(num_heads, val_dim, w_o.sh...  9.3 us
    dot_general x1, matrix products, feed_forward(): jnp.einsum('bcd,df->bcf', h_two, w_up, preferred_element_type=jnp.float32)  5.05 us
    dot_general x1, matrix products, project_heads(): jnp.einsum('bcd,dhe->bche', h_one, w_v.reshape(d_model, num_heads, val_di...  4.85 us
    dot_general x1, matrix products, feed_forward(): jnp.einsum('bcf,fd->bcd', activated, w_down, preferred_element_type=jnp.f...  3.37 us
  transfers between devices with their start and end apart: 2, of which 2 were waited for; matrix products, arithmetic and copies ran while one was open for 2% of the time, Pallas kernels for 0%

commit v1 on v0

--- a/solution.py
+++ b/solution.py
@@ -1,11 +1,19 @@
+import functools
+
 import jax
 import jax.numpy as jnp
 from jax import lax
+from jax.experimental import pallas as pl
+from jax.experimental.pallas import tpu as pltpu
 from jax.sharding import PartitionSpec as P
 
 NORM_EPS = 1e-5
 GROUP_EPS = 1e-6
 ROPE_BASE = 10000.0
+NUM_CHUNKS = 4
+MESH = pl.DeviceIdType.MESH
+F32 = jnp.float32
+BF16 = jnp.bfloat16
 
 
 def layer_norm(x_f32, norm_gain, norm_bias):
@@ -47,10 +55,8 @@
     return queries, keys, values, gates
 
 
-def mix_heads(queries, keys, values_f32, gates, state_in, log_gamma, w_o):
+def mix_heads(queries, keys, values_f32, gates, state_in, log_gamma):
     chunk_len = queries.shape[1]
-    num_heads = queries.shape[2]
-    val_dim = values_f32.shape[3]
     step_ids = jnp.arange(chunk_len)
     step_gap = step_ids[:, None] - step_ids[None, :]
     inner_decay = jnp.where(step_gap[None] >= 0, jnp.exp(jnp.maximum(step_gap, 0).astype(jnp.float32)[None] * log_gamma[:, None, None]), 0.0)
@@ -61,8 +67,7 @@
     centered = retained - row_mean
     variance = jnp.mean(centered * centered, axis=-1, keepdims=True)
     normed = centered * lax.rsqrt(variance + GROUP_EPS)
-    mixed = (jax.nn.silu(gates) * normed).astype(jnp.bfloat16)
-    return jnp.einsum('bche,hed->bcd', mixed, w_o.reshape(num_heads, val_dim, w_o.shape[1]), preferred_element_type=jnp.float32)
+    return (jax.nn.silu(gates) * normed).astype(jnp.bfloat16)
 
 
 def chunk_state(keys, values_f32, log_gamma):
@@ -72,16 +77,239 @@
     return jnp.einsum('bjhk,bjhe->bhke', keys.astype(jnp.float32) * key_decay[:, :, None], values_f32)
 
 
-def feed_forward(x_mid, ln2_gain, ln2_bias, w_up, w_down):
-    h_two = layer_norm(x_mid.astype(jnp.float32), ln2_gain, ln2_bias).astype(jnp.bfloat16)
-    activated = jax.nn.gelu(jnp.einsum('bcd,df->bcf', h_two, w_up, preferred_element_type=jnp.float32), approximate=False).astype(jnp.bfloat16)
-    return jnp.einsum('bcf,fd->bcd', activated, w_down, preferred_element_type=jnp.float32)
+def tail_kernel(z_ref, x_hbm, wo_hbm, wu_hbm, wd_hbm, gain_ref, bias_ref, out_ref,
+                wo, wu, wd, x_own, keep, act, h_all, x_mid,
+                pair_tx, pair_rx, far_tx, far_rx, near_tx, near_rx,
+                w_sem, x_sem,
+                pair_ss, pair_rs, far_ss, far_rs, near_ss, near_rs,
+                ag_ss, ag_rs, fw_ss, fw_rs, d2d_ss, d2d_rs):
+    nc = NUM_CHUNKS
+    rows, d_model = out_ref.shape
+    width = d_model // nc
+    half = width // 2
+    cls_rows = rows // 2
+    blk = cls_rows // 4
+    me = lax.axis_index('tp')
+    chip = lax.div(me, 2)
+    core = lax.rem(me, 2)
+    right = {'tp': lax.rem(chip + 1, 4) * 2 + core}
+    left = {'tp': lax.rem(chip + 3, 4) * 2 + core}
+    other = {'tp': chip * 2 + (1 - core)}
+    own_cls = pl.multiple_of(core * cls_rows, cls_rows)
+    oth_cls = pl.multiple_of((1 - core) * cls_rows, cls_rows)
+
+    def blk_at(k):
+        return pl.multiple_of(lax.rem(chip + k, 4) * blk, blk)
+
+    b_own, b_right, b_far, b_left = blk_at(0), blk_at(1), blk_at(2), blk_at(3)
+
+    def rdma(src, dst, ss, rs, dev):
+        return pltpu.make_async_remote_copy(src_ref=src, dst_ref=dst, send_sem=ss, recv_sem=rs, device_id=dev, device_id_type=MESH)
+
+    loads = {}
+    for j in range(nc):
+        cs = pl.ds(j * width, width)
+        loads['o', j] = pltpu.make_async_copy(wo_hbm.at[:, cs], wo.at[:, cs], w_sem.at[0, j])
+        loads['u', j] = pltpu.make_async_copy(wu_hbm.at[cs, :], wu.at[cs, :], w_sem.at[1, j])
+        loads['d', j] = pltpu.make_async_copy(wd_hbm.at[:, cs], wd.at[:, cs], w_sem.at[2, j])
+    x_load = pltpu.make_async_copy(x_hbm.at[pl.ds(own_cls + b_own, blk), :], x_own, x_sem)
+    loads['o', 0].start()
+    x_load.start()
+    for j in range(1, nc):
+        loads['o', j].start()
+    for j in range(nc):
+        loads['u', j].start()
+    for j in range(nc):
+        loads['d', j].start()
+
+    barrier = pltpu.get_barrier_semaphore()
+    for dev in (right, left, other):
+        pl.semaphore_signal(barrier, inc=1, device_id=dev, device_id_type=MESH)
+    pl.semaphore_wait(barrier, 3)
+
+    sends = []
+
+    def go(copy):
+        copy.start()
+        sends.append(copy)
+        return copy
+
+    def reduce_scatter(p, lhs_keep, lhs_send, w_ref, tag, finish):
+        near = {}
+
+        def compute(j):
+            loads[tag, j].wait()
+            cs = pl.ds(j * width, width)
+            part = jnp.dot(jnp.concatenate([lhs_send(), lhs_keep()], axis=0), w_ref[:, cs], preferred_element_type=F32)
+            pair_tx[p, :, cs] = part[:cls_rows].astype(BF16)
+            keep[:, cs] = part[cls_rows:]
+            go(rdma(pair_tx.at[p, :, cs], pair_rx.at[p, :, cs], pair_ss.at[p, j], pair_rs.at[p, j], other))
+
+        def pair(j):
+            cs = pl.ds(j * width, width)
+            rdma(pair_tx.at[p, :, cs], pair_rx.at[p, :, cs], pair_ss.at[p, j], pair_rs.at[p, j], other).wait_recv()
+            far = keep[pl.ds(b_far, blk), cs] + pair_rx[p, pl.ds(b_far, blk), cs].astype(F32)
+            far_tx[p, :, cs] = far.astype(BF16)
+            for s, dev in ((0, right), (1, left)):
+                hs = pl.ds(j * width + s * half, half)
+                go(rdma(far_tx.at[p, :, hs], far_rx.at[p, :, hs], far_ss.at[p, j, s], far_rs.at[p, j, s], dev))
+
+        def relay(j):
+            cs = pl.ds(j * width, width)
+            for s, dev, blk_id in ((0, right, b_right), (1, left, b_left)):
+                hs = pl.ds(j * width + s * half, half)
+                os = pl.ds(j * width + (1 - s) * half, half)
+                rdma(far_tx.at[p, :, hs], far_rx.at[p, :, hs], far_ss.at[p, j, s], far_rs.at[p, j, s], dev).wait_recv()
+                bs = pl.ds(blk_id, blk)
+                near_tx[p, s, :, hs] = (keep[bs, hs] + pair_rx[p, bs, hs].astype(F32) + far_rx[p, :, hs].astype(F32)).astype(BF16)
+                near_tx[p, s, :, os] = (keep[bs, os] + pair_rx[p, bs, os].astype(F32)).astype(BF16)
+                go(rdma(near_tx.at[p, s, :, cs], near_rx.at[p, s, :, cs], near_ss.at[p, j, s], near_rs.at[p, j, s], dev))
+
+        def final(j):
+            cs = pl.ds(j * width, width)
+            bs = pl.ds(b_own, blk)
+            total = keep[bs, cs] + pair_rx[p, bs, cs].astype(F32)
+            for s, dev in ((0, right), (1, left)):
+                rdma(near_tx.at[p, s, :, cs], near_rx.at[p, s, :, cs], near_ss.at[p, j, s], near_rs.at[p, j, s], dev).wait_recv()
+                total = total + near_rx[p, s, :, cs].astype(F32)
+            finish(j, total)
+
+        for t in range(nc + 6):
+            if t < nc:
+                compute(t)
+            if 0 <= t - 2 < nc:
+                pair(t - 2)
+            if 0 <= t - 4 < nc:
+                relay(t - 4)
+            if 0 <= t - 6 < nc:
+                final(t - 6)
+
+    def gather_send(p, buf, j):
+        rs = pl.ds(own_cls + b_own, blk)
+        cs = pl.ds(j * width, width)
+        for s, dev in ((0, right), (1, left)):
+            go(rdma(buf.at[rs, cs], buf.at[rs, cs], ag_ss.at[p, j, s], ag_rs.at[p, j, s], dev))
+        go(rdma(buf.at[rs, cs], buf.at[rs, cs], d2d_ss.at[p, j, 0], d2d_rs.at[p, j, 0], other))
+
+    def gather_forward(p, buf, j):
+        cs = pl.ds(j * width, width)
+        for s, dev, back, blk_id in ((0, right, left, b_left), (1, left, right, b_right)):
+            rs = pl.ds(own_cls + blk_id, blk)
+            hs = pl.ds(j * width + s * half, half)
+            rdma(buf.at[rs, cs], buf.at[rs, cs], ag_ss.at[p, j, s], ag_rs.at[p, j, s], dev).wait_recv()
+            go(rdma(buf.at[rs, hs], buf.at[rs, hs], fw_ss.at[p, j, s], fw_rs.at[p, j, s], dev))
+            go(rdma(buf.at[rs, cs], buf.at[rs, cs], d2d_ss.at[p, j, 1 + s], d2d_rs.at[p, j, 1 + s], other))
+
+    def gather_far(p, buf, j):
+        cs = pl.ds(j * width, width)
+        rs = pl.ds(own_cls + b_far, blk)
+        for s, dev in ((0, right), (1, left)):
+            hs = pl.ds(j * width + s * half, half)
+            rdma(buf.at[rs, hs], buf.at[rs, hs], fw_ss.at[p, j, s], fw_rs.at[p, j, s], dev).wait_recv()
+        go(rdma(buf.at[rs, cs], buf.at[rs, cs], d2d_ss.at[p, j, 3], d2d_rs.at[p, j, 3], other))
+
+    def gather_wait(p, buf, j):
+        cs = pl.ds(j * width, width)
+        for k, blk_id in enumerate((b_own, b_left, b_right, b_far)):
+            rs = pl.ds(oth_cls + blk_id, blk)
+            rdma(buf.at[rs, cs], buf.at[rs, cs], d2d_ss.at[p, j, k], d2d_rs.at[p, j, k], other).wait_recv()
+
+    x_load.wait()
+
+    def finish_u(j, total):
+        cs = pl.ds(j * width, width)
+        x_mid[:, cs] = (x_own[:, cs].astype(F32) + total.astype(BF16).astype(F32)).astype(BF16)
+
+    reduce_scatter(0, lambda: z_ref[pl.ds(own_cls, cls_rows), :], lambda: z_ref[pl.ds(oth_cls, cls_rows), :], wo, 'o', finish_u)
+
+    x1 = x_mid[...].astype(F32)
+    mean = jnp.mean(x1, axis=-1, keepdims=True)
+    centered = x1 - mean
+    var = jnp.mean(centered * centered, axis=-1, keepdims=True)
+    h_own = (centered * lax.rsqrt(var + NORM_EPS) * gain_ref[...] + bias_ref[...]).astype(BF16)
+    h_all[pl.ds(own_cls + b_own, blk), :] = h_own
+    for j in range(nc):
+        gather_send(0, h_all, j)
+
+    up = None
+    for j in range(nc):
+        gather_forward(0, h_all, j)
+        if j > 0:
+            gather_far(0, h_all, j - 1)
+    gather_far(0, h_all, nc - 1)
+    for j in range(nc):
+        gather_wait(0, h_all, j)
+        loads['u', j].wait()
+        cs = pl.ds(j * width, width)
+        part = jnp.dot(h_all[:, cs], wu[cs, :], preferred_element_type=F32)
+        up = part if up is None else up + part
+    act[...] = (0.5 * up * (1.0 + lax.erf(up * (0.5 ** 0.5)))).astype(BF16)
+
+    def finish_f(j, total):
+        cs = pl.ds(j * width, width)
+        x2 = x_mid[:, cs].astype(F32) + total.astype(BF16).astype(F32)
+        out_ref[pl.ds(own_cls + b_own, blk), cs] = x2.astype(BF16)
+        gather_send(1, out_ref, j)
+
+    reduce_scatter(1, lambda: act[pl.ds(own_cls, cls_rows), :], lambda: act[pl.ds(oth_cls, cls_rows), :], wd, 'd', finish_f)
+    for j in range(nc):
+        gather_forward(1, out_ref, j)
+        if j > 0:
+            gather_far(1, out_ref, j - 1)
+    gather_far(1, out_ref, nc - 1)
+    for j in range(nc):
+        gather_wait(1, out_ref, j)
+    for copy in sends:
+        copy.wait_send()
+
+
+def tail(z, x2d, w_o, w_up, w_down, gain, bias):
+    rows, d_model = x2d.shape
+    inner = z.shape[1]
+    ffn = w_up.shape[1]
+    nc = NUM_CHUNKS
+    blk = rows // 8
+    dma = pltpu.SemaphoreType.DMA
+    vmem = pl.BlockSpec(memory_space=pltpu.VMEM)
+    hbm = pl.BlockSpec(memory_space=pl.ANY)
+    return pl.pallas_call(
+        tail_kernel,
+        out_shape=jax.ShapeDtypeStruct((rows, d_model), BF16),
+        in_specs=[vmem, hbm, hbm, hbm, hbm, vmem, vmem],
+        out_specs=vmem,
+        scratch_shapes=[
+            pltpu.VMEM((inner, d_model), BF16),
+            pltpu.VMEM((d_model, ffn), BF16),
+            pltpu.VMEM((ffn, d_model), BF16),
+            pltpu.VMEM((blk, d_model), BF16),
+            pltpu.VMEM((rows // 2, d_model), F32),
+            pltpu.VMEM((rows, ffn), BF16),
+            pltpu.VMEM((rows, d_model), BF16),
+            pltpu.VMEM((blk, d_model), BF16),
+            pltpu.VMEM((2, rows // 2, d_model), BF16),
+            pltpu.VMEM((2, rows // 2, d_model), BF16),
+            pltpu.VMEM((2, blk, d_model), BF16),
+            pltpu.VMEM((2, blk, d_model), BF16),
+            pltpu.VMEM((2, 2, blk, d_model), BF16),
+            pltpu.VMEM((2, 2, blk, d_model), BF16),
+            dma((3, nc)),
+            dma,
+            dma((2, nc)), dma((2, nc)),
+            dma((2, nc, 2)), dma((2, nc, 2)),
+            dma((2, nc, 2)), dma((2, nc, 2)),
+            dma((2, nc, 2)), dma((2, nc, 2)),
+            dma((2, nc, 2)), dma((2, nc, 2)),
+            dma((2, nc, 4)), dma((2, nc, 4)),
+        ],
+        compiler_params=pltpu.CompilerParams(collective_id=0, has_side_effects=True, vmem_limit_bytes=60 * 1024 * 1024),
+        name='tail',
+    )(z, x2d, w_o, w_up, w_down, gain, bias)
 
 
 def solution(mesh):
     def local_layer(x_in, start_pos, kv_state, ln1_gain, ln1_bias, w_q, w_k, w_v, w_g, w_o, ln2_gain, ln2_bias, w_up, w_down):
         local_heads = kv_state.shape[1]
-        chunk_len = x_in.shape[1]
+        batch, chunk_len, d_model = x_in.shape
         head_ids = lax.axis_index('tp') * local_heads + jnp.arange(local_heads)
         log_gamma = head_log_decay(head_ids)
         x_f32 = x_in.astype(jnp.float32)
@@ -89,14 +317,11 @@
         cos_t, sin_t = rope_tables(start_pos, chunk_len, kv_state.shape[2])
         queries, keys, values, gates = project_heads(h_one, cos_t, sin_t, w_q, w_k, w_v, w_g, local_heads)
         values_f32 = values.astype(jnp.float32)
-        attn_part = mix_heads(queries, keys, values_f32, gates, kv_state, log_gamma, w_o).astype(jnp.bfloat16)
+        mixed = mix_heads(queries, keys, values_f32, gates, kv_state, log_gamma)
         new_state = jnp.exp(chunk_len * log_gamma)[:, None, None] * kv_state + chunk_state(keys, values_f32, log_gamma)
-        attn_out = lax.psum(attn_part, 'tp')
-        x_mid = (x_f32 + attn_out.astype(jnp.float32)).astype(jnp.bfloat16)
-        ffn_part = feed_forward(x_mid, ln2_gain, ln2_bias, w_up, w_down).astype(jnp.bfloat16)
-        ffn_out = lax.psum(ffn_part, 'tp')
-        x_out = (x_mid.astype(jnp.float32) + ffn_out.astype(jnp.float32)).astype(jnp.bfloat16)
-        return x_out, new_state
+        rows = batch * chunk_len
+        x_out = tail(mixed.reshape(rows, -1), x_in.reshape(rows, d_model), w_o, w_up, w_down, ln2_gain.reshape(1, -1), ln2_bias.reshape(1, -1))
+        return x_out.reshape(x_in.shape), new_state
 
     in_specs = (P('dp', None, None), P('dp'), P('dp', 'tp', None, None), P(), P(), P(None, 'tp'), P(None, 'tp'), P(None, 'tp'), P(None, 'tp'), P('tp', None), P(), P(), P(None, 'tp'), P('tp', None))
     out_specs = (P('dp', None, None), P('dp', 'tp', None, None))

time: 166 us -> 89.1 us (0.54)
  waiting for transfers between devices: 111 us -> 0 us
  Pallas kernels: 0 us -> 59.8 us
  between operations: 14.3 us -> 0.81 us
  matrix products: 27.7 us -> 17.3 us
  other arithmetic: 9.44 us -> 6.81 us
  local copies, waits for them, and re-layouts: 1.77 us -> 4.18 us
    psum x2 -> x0, waiting for transfers between devices: 111 us -> none  [the longest x1 58.2 us: local_layer(): attn_out = lax.psum(attn_part, 'tp')]
    pallas_call x0 -> x1, Pallas kernels: none -> 59.8 us  [tail(): pl.pallas_call(tail_kernel, out_shape=jax.ShapeDtypeStruct((rows, d_model...]
    dot_general x3 -> x1, matrix products: 17.7 us -> 4.92 us  [project_heads(): jnp.einsum('bcd,dhe->bche', h_one, w_g.reshape(d_model, num_heads, val_di...]
    convert_element_type x1 -> x0, other arithmetic: 2.44 us -> none  [local_layer(): (x_mid.astype(jnp.float32) + ffn_out.astype(jnp.float32)).astype(jnp.bflo...]
    unnamed x24 -> x20, local copies, waits for them, and re-layouts: 1.77 us -> 3.91 us
    dot_general x1, matrix products: 0.42 us -> 2.3 us  [mix_heads(): jnp.einsum('bhcj,bjhe->bche', scores, values_f32)]
    reduce_sum x2 -> x1, other arithmetic: 3.22 us -> 1.46 us  [layer_norm(): row_mean = jnp.mean(x_f32, axis=-1, keepdims=True)]
  transfers between devices with their start and end apart: 2 -> 0, of which waited for: 2 -> 0; matrix products, arithmetic and copies ran while one was open for 2% -> 0% of each run, Pallas kernels for 0% -> 0%
where the time goes in v1:
time: 89.1 us; the launch traced here: 88.8 us
  Pallas kernels  59.8 us (67%)
  matrix products  17.3 us (19%)
  other arithmetic  6.81 us (8%)
  local copies, waits for them, and re-layouts  4.18 us (5%)
    pallas_call x1, Pallas kernels, tail(): pl.pallas_call(tail_kernel, out_shape=jax.ShapeDtypeStruct((rows, d_model...  59.8 us
    dot_general x1, matrix products, project_heads(): jnp.einsum('bcd,dhe->bche', h_one, w_v.reshape(d_model, num_heads, val_di...  5.55 us
    dot_general x1, matrix products, project_heads(): jnp.einsum('bcd,dhe->bche', h_one, w_g.reshape(d_model, num_heads, val_di...  4.92 us
    unnamed x20, local copies, waits for them, and re-layouts  3.91 us
    dot_general x1, matrix products, mix_heads(): jnp.einsum('bhcj,bjhe->bche', scores, values_f32)  2.3 us
    dot_general x1, matrix products, chunk_state(): jnp.einsum('bjhk,bjhe->bhke', keys.astype(jnp.float32) * key_decay[:, :,...  1.89 us

profile of v1, /device:TPU:81, one launch (start us, length us, event | category | flops | bytes accessed | tf_op | source)
XLA Modules:
  0.0 88.8 jit_solution(12445115718869211148)
XLA Ops:
  0.6 0.0 copy-start
  0.6 0.0 copy-start.7
  0.7 0.0 copy-start.8
  0.7 0.5 multiply_exponential_fusion.2
  1.2 0.7 add_convert_fusion.1
  1.9 1.5 %convert_reduce_fusion = f32[2,64]{1,0:T(2,128)S(1)} fusion(bf16[2,64,4096]{2,1,0:T(8,128)(2,1)} %param.14), kind=kLoop, calls=%fused_computation.13 | loop fusion | flops 1048448 | bytes 1049088 | tf_op jit(solution)/shard_map/reduce_sum | solution.py:20
  3.4 1.7 %fusion.10 = f32[2,64]{1,0:T(2,128)S(1)} fusion(bf16[2,64,4096]{2,1,0:T(8,128)(2,1)} %param.14, f32[2,64]{1,0:T(2,128)S(1)} %broadcast_multiply_fusion.1), kind=kLoop, calls=%fused_computation.16 | loop fusion | flops 2097024 | bytes 1049600 | tf_op jit(solution)/shard_map/reduce_sum | solution.py:22
  5.1 0.1 multiply_exponential_fusion
  5.2 0.7 exponential_select_fusion
  5.9 0.3 multiply_cosine_fusion
  6.2 0.0 copy-done
  6.2 0.0 copy-done.7
  6.2 0.0 copy-done.8
  6.2 0.0 copy-start.5
  6.2 5.6 %fusion.16 = bf16[2,64,2,512]{3,1,2,0:T(8,128)(2,1)} fusion(bf16[512,2,8,512]{3,2,1,0:T(8,128)(2,1)} %bitcast.68, bf16[2,64,4096]{2,1,0:T(8,128)(2,1)S(1)} %copy-done, f32[4096]{0:T(1024)S(1)} %copy-done.7, f32[4096]{0:T(1024)S(1)} %copy-done.8, f32[2,64]{1,0:T(2,128)S(1)} %add_rsqrt_fusion.1, f32[2,64]{1,0:T(2,128)S(1)} %broadcast_multiply_fusion.1), kind=kOutput, calls=%fused_computation.25 | convolution fusion | flops 1077018624 | bytes 9733120 | tf_op jit(solution)/shard_map/bcd,dhe->bche/dot_general | solution.py:53
  11.8 0.0 copy-done.5
  11.8 0.0 copy-start.6
  11.8 0.8 fusion.6
  12.6 1.4 %copy-done.6 = bf16[4096,512]{1,0:T(8,128)(2,1)S(1)} copy-done((bf16[4096,512]{1,0:T(8,128)(2,1)S(1)}, bf16[4096,512]{1,0:T(8,128)(2,1)}, u32[]{:S(2)}) %copy-start.6) | copy-done | bytes 4194328
  14.0 0.0 copy-start.1
  14.0 0.8 fusion.4
  14.7 0.1 multiply_subtract_fusion
  14.8 0.7 copy-done.1
  15.6 1.1 %fusion.14 = f32[2,64,2,512]{3,1,2,0:T(8,128)} fusion(f32[2,2,256,512]{3,2,1,0:T(8,128)S(1)} %copy-done.1, f32[64,2]{0,1:T(2,128)S(1)} %get-tuple-element.11, bf16[2,64,2,128]{3,1,2,0:T(8,128)(2,1)S(1)} %get-tuple-element.6, bf16[2,64,2,128]{3,1,2,0:T(8,128)(2,1)S(1)} %get-tuple-element.7), kind=kOutput, calls=%fused_computation.22 | convolution fusion | flops 67502080 | bytes 2753024 | tf_op jit(solution)/shard_map/bchk,bhke->bche/dot_general | solution.py:65
  16.7 2.3 %fusion.40 = (f32[2,64,2]{1,2,0:T(2,128)S(1)}, f32[2,64,2,512]{3,1,2,0:T(8,128)}) fusion(f32[2,64,2,512]{3,1,2,0:T(8,128)} %fusion.14, bf16[2,64,2,512]{3,1,2,0:T(8,128)(2,1)} %fusion.16, bf16[2,64,2,128]{3,1,2,0:T(8,128)(2,1)S(1)} %get-tuple-element.6, bf16[2,64,2,128]{3,1,2,0:T(8,128)(2,1)S(1)} %get-tuple-element.7, ...), kind=kOutput, calls=%fused_computation.65 | convolution fusion | flops 25902848 | bytes 1737728 | tf_op jit(solution)/shard_map/bhcj,bjhe->bche/dot_general | solution.py:65
  19.0 1.2 %multiply_reduce_fusion = f32[2,64,2]{1,2,0:T(2,128)S(1)} fusion(f32[2,64,2,512]{3,1,2,0:T(8,128)} %get-tuple-element.13, f32[2,64,2]{1,2,0:T(2,128)S(1)} %broadcast_multiply_fusion), kind=kLoop, calls=%fused_computation.29 | loop fusion | flops 392960 | bytes 526336 | tf_op jit(solution)/shard_map/reduce_sum | solution.py:68
  20.2 4.9 %multiply_convert_fusion = bf16[2,64,2,512]{3,1,2,0:T(8,128)(2,1)S(1)} fusion(bf16[512,2,8,512]{3,2,1,0:T(8,128)(2,1)} %bitcast.69, f32[2,64,2,512]{3,1,2,0:T(8,128)} %get-tuple-element.13, f32[2,64,2]{1,2,0:T(2,128)S(1)} %add_rsqrt_fusion, f32[2,64,2]{1,2,0:T(2,128)S(1)} %broadcast_multiply_fusion, bf16[2,64,4096]{2,1,0:T(8,128)(2,1)S(1)} %copy-done, ...), kind=kOutput, calls=%fused_computation.28 | convolution fusion | flops 1077936128 | bytes 10259456 | tf_op jit(solution)/shard_map/bcd,dhe->bche/dot_general | solution.py:54
  25.1 0.3 copy.20
  25.4 0.7 copy.26
  26.2 0.0 copy-start.3
  26.2 0.0 copy-start.4
  26.2 59.8 %tail.1 = bf16[128,4096]{1,0:T(8,128)(2,1)} custom-call(bf16[128,1024]{1,0:T(8,128)(2,1)} %bitcast.64, bf16[128,4096]{1,0:T(8,128)(2,1)} %bitcast.62, bf16[1024,4096]{1,0:T(8,128)(2,1)} %wo_hbm.1, bf16[4096,1024]{1,0:T(8,128)(2,1)} %wu_hbm.1, bf16[1024,4096]{1,0:T(8,128)(2,1)} %wd_hbm.1, f32[1,4096]{1,0:T(1,128)} %bitcast.66, f32[1,4096]{1,0:T(1,128)} %bitcast.67), custom_call_target="tpu_custom_call" | custom-call | tf_op jit(solution)/shard_map/tail/pallas_call | solution.py:275
  85.9 0.0 copy-done.3
  85.9 0.0 copy-done.4
  85.9 0.0 copy-start.2
  86.0 1.9 %multiply_add_fusion = f32[2,2,256,512]{3,2,1,0:T(8,128)} fusion(f32[2,2,256,512]{3,2,1,0:T(8,128)S(1)} %copy-done.1, bf16[2,64,2,512]{3,1,2,0:T(8,128)(2,1)S(1)} %copy-done.3, f32[2]{0:T(128)S(1)} %copy-done.4, f32[64,2]{0,1:T(2,128)S(1)} %get-tuple-element.10, f32[2,64,2,128]{3,1,2,0:T(8,128)S(1)} %get-tuple-element.3, ...), kind=kOutput, calls=%fused_computation.20 | convolution fusion | flops 68485120 | bytes 4719112 | tf_op jit(solution)/shard_map/bjhk,bjhe->bhke/dot_general | solution.py:77
  87.8 0.0 copy-done.2
  87.8 1.0 %copy.48 = bf16[2,64,4096]{2,1,0:T(8,128)(2,1)} copy(bf16[2,64,4096]{2,1,0:T(8,128)(2,1)S(1)} %bitcast.63) | data formatting | bytes 2097152
  (8 shorter events, 0.1 us)
Async XLA Ops:
  0.6 5.6 %copy-start = (bf16[2,64,4096]{2,1,0:T(8,128)(2,1)S(1)}, bf16[2,64,4096]{2,1,0:T(8,128)(2,1)}, u32[]{:S(2)}) copy-start(bf16[2,64,4096]{2,1,0:T(8,128)(2,1)} %param.14) | copy-start | bytes 3145732
  0.6 5.6 %copy-start.7 = (f32[4096]{0:T(1024)S(1)}, f32[4096]{0:T(1024)}, u32[]{:S(2)}) copy-start(f32[4096]{0:T(1024)} %param.18) | copy-start | bytes 49156
  0.7 5.6 %copy-start.8 = (f32[4096]{0:T(1024)S(1)}, f32[4096]{0:T(1024)}, u32[]{:S(2)}) copy-start(f32[4096]{0:T(1024)} %param.17) | copy-start | bytes 49156
  6.2 5.6 %copy-start.5 = (bf16[4096,512]{1,0:T(8,128)(2,1)S(1)}, bf16[4096,512]{1,0:T(8,128)(2,1)}, u32[]{:S(2)}) copy-start(bf16[4096,512]{1,0:T(8,128)(2,1)} %param.19) | copy-start | bytes 12582916
  11.8 2.2 %copy-start.6 = (bf16[4096,512]{1,0:T(8,128)(2,1)S(1)}, bf16[4096,512]{1,0:T(8,128)(2,1)}, u32[]{:S(2)}) copy-start(bf16[4096,512]{1,0:T(8,128)(2,1)} %param.20) | copy-start | bytes 12582916
  14.0 1.6 %copy-start.1 = (f32[2,2,256,512]{3,2,1,0:T(8,128)S(1)}, f32[2,2,256,512]{3,2,1,0:T(8,128)}, u32[]{:S(2)}) copy-start(f32[2,2,256,512]{3,2,1,0:T(8,128)} %param.16) | copy-start | bytes 6291460
  26.2 59.8 %copy-start.3 = (bf16[2,64,2,512]{3,1,2,0:T(8,128)(2,1)S(1)}, bf16[2,64,2,512]{3,1,2,0:T(8,128)(2,1)}, u32[]{:S(2)}) copy-start(bf16[2,64,2,512]{3,1,2,0:T(8,128)(2,1)} %fusion.16) | copy-start | bytes 786436
  26.2 59.8 %copy-start.4 = (f32[2]{0:T(128)S(1)}, f32[2]{0:T(128)}, u32[]{:S(2)}) copy-start(f32[2]{0:T(128)} %get-tuple-element.14) | copy-start | bytes 28
  85.9 1.9 %copy-start.2 = (bf16[128,4096]{1,0:T(8,128)(2,1)S(1)}, bf16[128,4096]{1,0:T(8,128)(2,1)}, u32[]{:S(2)}) copy-start(bf16[128,4096]{1,0:T(8,128)(2,1)} %tail.1) | copy-start | bytes 3145732

commit v2 on v1

v2 whole, which is shorter than its diff:
```python
import jax
import jax.numpy as jnp
import numpy as np
from jax import lax
from jax.experimental import pallas as pl
from jax.experimental.pallas import tpu as pltpu
from jax.sharding import PartitionSpec as P

NORM_EPS = 1e-5
GROUP_EPS = 1e-6
ROPE_BASE = 10000.0
NUM_CHUNKS = 4
SCHEDULE = (
    [('compute', 0), ('compute', 1), ('compute', 2), ('pair', 0), ('compute', 3), ('pair', 1), ('pair', 2), ('pair', 3)]
    + [('relay', j) for j in range(NUM_CHUNKS)] + [('final', j) for j in range(NUM_CHUNKS)]
)
MESH = pl.DeviceIdType.MESH
F32 = jnp.float32
BF16 = jnp.bfloat16


def head_kernel(pos_ref, lg_ref, freq_ref, gain_ref, bias_ref, x_hbm, s_hbm, wq_hbm, wk_hbm, wv_hbm, wg_hbm, z_ref, s_out,
                x, h, wq, wk, wv, wg, s_in, s_new, q, k, v, o, sem, out_sem):
    batch, heads, key_dim, val_dim = s_hbm.shape
    rows, d_model = x.shape
    chunk = rows // batch
    half = key_dim // 2
    me = lax.axis_index('tp')

    loads = {}

    def add(name, src, dst):
        loads[name] = pltpu.make_async_copy(src, dst, sem.at[len(loads)])

    add('x', x_hbm, x)
    for name, src, dst, pieces in (('q', wq_hbm, wq, 2), ('k', wk_hbm, wk, 2), ('s', s_hbm, s_in, 1), ('v', wv_hbm, wv, 4), ('g', wg_hbm, wg, 4)):
        if pieces == 1:
            add((name, 0), src, dst)
        else:
            for i in range(pieces):
                rs = pl.ds(i * (d_model // pieces), d_model // pieces)
                add((name, i), src.at[rs, :], dst.at[rs, :])
    order = list(loads)
    state = {'next': 0}

    def issue(count):
        for name in order[state['next']:state['next'] + count]:
            loads[name].start()
        state['next'] += count

    def wait(name, count=1):
        with jax.named_scope('load'):
            loads[name].wait()
        issue(count)

    issue(5)

    with jax.named_scope('tables'):
        token = lax.broadcasted_iota(jnp.int32, (chunk, half), 0)
        pos = jnp.concatenate([token + pos_ref[b] for b in range(batch)], axis=0)
        angles = pos.astype(F32) * freq_ref[...]
        cos_t = jnp.cos(angles)
        sin_t = jnp.sin(angles)

    wait('x', 0)
    with jax.named_scope('ln1'):
        step = 16
        for r in range(0, rows, step):
            rs = pl.ds(r, step)
            xf = x[rs, :].astype(F32)
            mean = jnp.mean(xf, axis=-1, keepdims=True)
            centered = xf - mean
            var = jnp.mean(centered * centered, axis=-1, keepdims=True)
            h[rs, :] = (centered * lax.rsqrt(var + NORM_EPS) * gain_ref[...] + bias_ref[...]).astype(BF16)

    def project(name, w, pieces):
        total = None
        for i in range(pieces):
            wait((name, i))
            with jax.named_scope(f'dot_{name}{i}'):
                rs = pl.ds(i * (d_model // pieces), d_model // pieces)
                part = jnp.dot(h[:, rs], w[rs, :], preferred_element_type=F32)
                total = part if total is None else total + part
        return total

    def rotate(dst, raw, scale):
        for n in range(heads):
            a = raw[:, n * key_dim:n * key_dim + half]
            b = raw[:, n * key_dim + half:(n + 1) * key_dim]
            dst[:, pl.ds(n * key_dim, half)] = ((a * cos_t - b * sin_t) * scale).astype(BF16)
            dst[:, pl.ds(n * key_dim + half, half)] = ((b * cos_t + a * sin_t) * scale).astype(BF16)

    rotate(q, project('q', wq, 2), 1.0)
    rotate(k, project('k', wk, 2), key_dim ** -0.5)
    wait(('s', 0))
    v[...] = project('v', wv, 4).astype(BF16)

    row = lax.broadcasted_iota(jnp.int32, (chunk, chunk), 0)
    col = lax.broadcasted_iota(jnp.int32, (chunk, chunk), 1)
    gap = jnp.maximum(row - col, 0).astype(F32)
    nth = lax.broadcasted_iota(jnp.int32, (chunk, 1), 0).astype(F32)

    def split(a):
        hi = a.astype(BF16)
        return hi, (a - hi.astype(F32)).astype(BF16)

    outs = []
    for n in range(heads):
        log_gamma = lg_ref[me * heads + n]
        inner = jnp.where(row >= col, jnp.exp(gap * log_gamma), 0.0)
        q_decay = jnp.exp((nth + 1.0) * log_gamma)
        k_decay = jnp.exp((chunk - 1.0 - nth) * log_gamma)
        s_decay = jnp.exp(jnp.full((1, val_dim), float(chunk), F32) * log_gamma)
        for b in range(batch):
            with jax.named_scope(f'mix{n}{b}'):
                bs = pl.ds(b * chunk, chunk)
                qb = q[bs, pl.ds(n * key_dim, key_dim)]
                kb = k[bs, pl.ds(n * key_dim, key_dim)]
                vb = v[bs, pl.ds(n * val_dim, val_dim)]
                v2 = jnp.concatenate([vb, vb], axis=0)
                scores = lax.dot_general(qb, kb, (((1,), (1,)), ((), ())), preferred_element_type=F32) * inner
                s_old = s_in[b, n]
                s_hi, s_lo = split(s_old)
                cross = jnp.dot(qb, s_hi, preferred_element_type=F32) + jnp.dot(qb, s_lo, preferred_element_type=F32)
                ret = jnp.dot(jnp.concatenate(split(scores), axis=1), v2, preferred_element_type=F32) + cross * q_decay
                mean = jnp.mean(ret, axis=-1, keepdims=True)
                centered = ret - mean
                var = jnp.mean(centered * centered, axis=-1, keepdims=True)
                o[bs, pl.ds(n * val_dim, val_dim)] = centered * lax.rsqrt(var + GROUP_EPS)
                kd = jnp.concatenate(split(kb.astype(F32) * k_decay), axis=0)
                s_new[b, n] = s_old * s_decay + lax.dot_general(kd, v2, (((0,), (0,)), ((), ())), preferred_element_type=F32)
                out = pltpu.make_async_copy(s_new.at[b, n], s_out.at[b, n], out_sem.at[b, n])
                out.start()
                outs.append(out)

    gates = project('g', wg, 4)
    with jax.named_scope('gate'):
        z_ref[...] = (gates * jax.nn.sigmoid(gates) * o[...]).astype(BF16)
    for out in outs:
        out.wait()


def head(pos, log_gamma, freq, gain, bias, x2d, kv_state, w_q, w_k, w_v, w_g):
    rows, d_model = x2d.shape
    batch, heads, key_dim, val_dim = kv_state.shape
    dma = pltpu.SemaphoreType.DMA
    vmem = pl.BlockSpec(memory_space=pltpu.VMEM)
    smem = pl.BlockSpec(memory_space=pltpu.SMEM)
    hbm = pl.BlockSpec(memory_space=pl.ANY)
    return pl.pallas_call(
        head_kernel,
        out_shape=(jax.ShapeDtypeStruct((rows, heads * val_dim), BF16), jax.ShapeDtypeStruct(kv_state.shape, F32)),
        in_specs=[smem, smem, vmem, vmem, vmem] + [hbm] * 6,
        out_specs=(vmem, hbm),
        scratch_shapes=[
            pltpu.VMEM((rows, d_model), BF16),
            pltpu.VMEM((rows, d_model), BF16),
            pltpu.VMEM(w_q.shape, BF16),
            pltpu.VMEM(w_k.shape, BF16),
            pltpu.VMEM(w_v.shape, BF16),
            pltpu.VMEM(w_g.shape, BF16),
            pltpu.VMEM(kv_state.shape, F32),
            pltpu.VMEM(kv_state.shape, F32),
            pltpu.VMEM((rows, heads * key_dim), BF16),
            pltpu.VMEM((rows, heads * key_dim), BF16),
            pltpu.VMEM((rows, heads * val_dim), BF16),
            pltpu.VMEM((rows, heads * val_dim), F32),
            dma((16,)),
            dma((batch, heads)),
        ],
        compiler_params=pltpu.CompilerParams(vmem_limit_bytes=60 * 1024 * 1024),
        name='head',
    )(pos, log_gamma, freq, gain, bias, x2d, kv_state, w_q, w_k, w_v, w_g)


def tail_kernel(z_ref, x_hbm, wo_hbm, wu_hbm, wd_hbm, gain_ref, bias_ref, out_ref,
                wo, wu, wd, x_own, keep, act, h_all, x_mid,
                pair_tx, pair_rx, far_tx, far_rx, near_tx, near_rx,
                w_sem, x_sem,
                pair_ss, pair_rs, far_ss, far_rs, near_ss, near_rs,
                ag_ss, ag_rs, fw_ss, fw_rs, d2d_ss, d2d_rs):
    nc = NUM_CHUNKS
    rows, d_model = out_ref.shape
    width = d_model // nc
    half = width // 2
    cls_rows = rows // 2
    blk = cls_rows // 4
    me = lax.axis_index('tp')
    chip = lax.div(me, 2)
    core = lax.rem(me, 2)
    right = {'tp': lax.rem(chip + 1, 4) * 2 + core}
    left = {'tp': lax.rem(chip + 3, 4) * 2 + core}
    other = {'tp': chip * 2 + (1 - core)}
    own_cls = pl.multiple_of(core * cls_rows, cls_rows)
    oth_cls = pl.multiple_of((1 - core) * cls_rows, cls_rows)

    def blk_at(k):
        return pl.multiple_of(lax.rem(chip + k, 4) * blk, blk)

    b_own, b_right, b_far, b_left = blk_at(0), blk_at(1), blk_at(2), blk_at(3)

    def rdma(src, dst, ss, rs, dev):
        return pltpu.make_async_remote_copy(src_ref=src, dst_ref=dst, send_sem=ss, recv_sem=rs, device_id=dev, device_id_type=MESH)

    loads = {}
    for j in range(nc):
        cs = pl.ds(j * width, width)
        loads['o', j] = pltpu.make_async_copy(wo_hbm.at[:, cs], wo.at[:, cs], w_sem.at[0, j])
        loads['u', j] = pltpu.make_async_copy(wu_hbm.at[cs, :], wu.at[cs, :], w_sem.at[1, j])
        loads['d', j] = pltpu.make_async_copy(wd_hbm.at[:, cs], wd.at[:, cs], w_sem.at[2, j])
    x_load = pltpu.make_async_copy(x_hbm.at[pl.ds(own_cls + b_own, blk), :], x_own, x_sem)
    x_load.start()
    for j in range(nc):
        loads['o', j].start()

    barrier = pltpu.get_barrier_semaphore()
    for dev in (right, left, other):
        pl.semaphore_signal(barrier, inc=1, device_id=dev, device_id_type=MESH)
    with jax.named_scope('barrier'):
        pl.semaphore_wait(barrier, 3)

    sends = []

    def go(copy):
        copy.start()
        sends.append(copy)
        return copy

    def reduce_scatter(p, lhs_keep, lhs_send, w_ref, tag, finish):
        near = {}

        def compute(j):
            loads[tag, j].wait()
            if p == 0:
                loads['u', j].start()
            cs = pl.ds(j * width, width)
            part = jnp.dot(jnp.concatenate([lhs_send(), lhs_keep()], axis=0), w_ref[:, cs], preferred_element_type=F32)
            pair_tx[p, :, cs] = part[:cls_rows].astype(BF16)
            keep[:, cs] = part[cls_rows:]
            go(rdma(pair_tx.at[p, :, cs], pair_rx.at[p, :, cs], pair_ss.at[p, j], pair_rs.at[p, j], other))

        def pair(j):
            cs = pl.ds(j * width, width)
            rdma(pair_tx.at[p, :, cs], pair_rx.at[p, :, cs], pair_ss.at[p, j], pair_rs.at[p, j], other).wait_recv()
            far = keep[pl.ds(b_far, blk), cs] + pair_rx[p, pl.ds(b_far, blk), cs].astype(F32)
            far_tx[p, :, cs] = far.astype(BF16)
            for s, dev in ((0, right), (1, left)):
                hs = pl.ds(j * width + s * half, half)
                go(rdma(far_tx.at[p, :, hs], far_rx.at[p, :, hs], far_ss.at[p, j, s], far_rs.at[p, j, s], dev))
            for s, dev, blk_id in ((0, right, b_right), (1, left, b_left)):
                hs = pl.ds(j * width + (1 - s) * half, half)
                bs = pl.ds(blk_id, blk)
                near_tx[p, s, :, hs] = (keep[bs, hs] + pair_rx[p, bs, hs].astype(F32)).astype(BF16)
                go(rdma(near_tx.at[p, s, :, hs], near_rx.at[p, s, :, hs], near_ss.at[p, j, s, 0], near_rs.at[p, j, s, 0], dev))

        def relay(j):
            for s, dev, blk_id in ((0, right, b_right), (1, left, b_left)):
                hs = pl.ds(j * width + s * half, half)
                bs = pl.ds(blk_id, blk)
                rdma(far_tx.at[p, :, hs], far_rx.at[p, :, hs], far_ss.at[p, j, s], far_rs.at[p, j, s], dev).wait_recv()
                near_tx[p, s, :, hs] = (keep[bs, hs] + pair_rx[p, bs, hs].astype(F32) + far_rx[p, :, hs].astype(F32)).astype(BF16)
                go(rdma(near_tx.at[p, s, :, hs], near_rx.at[p, s, :, hs], near_ss.at[p, j, s, 1], near_rs.at[p, j, s, 1], dev))

        def final(j):
            cs = pl.ds(j * width, width)
            bs = pl.ds(b_own, blk)
            total = keep[bs, cs] + pair_rx[p, bs, cs].astype(F32)
            for s, dev in ((0, right), (1, left)):
                for i, off in ((0, (1 - s) * half), (1, s * half)):
                    hs = pl.ds(j * width + off, half)
                    rdma(near_tx.at[p, s, :, hs], near_rx.at[p, s, :, hs], near_ss.at[p, j, s, i], near_rs.at[p, j, s, i], dev).wait_recv()
                total = total + near_rx[p, s, :, cs].astype(F32)
            finish(j, total)

        for name, lag in SCHEDULE:
            with jax.named_scope(f'{name}{p}{lag}'):
                {'compute': compute, 'pair': pair, 'relay': relay, 'final': final}[name](lag)

    def gather_send(p, buf, js):
        rs = pl.ds(own_cls + b_own, blk)
        for i in (0, 1):
            for j in js:
                for s, dev in ((0, right), (1, left)):
                    hs = pl.ds(j * width + (s if i == 0 else 1 - s) * half, half)
                    go(rdma(buf.at[rs, hs], buf.at[rs, hs], ag_ss.at[p, j, s, i], ag_rs.at[p, j, s, i], dev))
        for j in js:
            cs = pl.ds(j * width, width)
            go(rdma(buf.at[rs, cs], buf.at[rs, cs], d2d_ss.at[p, j, 0], d2d_rs.at[p, j, 0], other))

    def gather_forward(p, buf, j):
        for s, dev, blk_id in ((0, right, b_left), (1, left, b_right)):
            rs = pl.ds(own_cls + blk_id, blk)
            hs = pl.ds(j * width + s * half, half)
            rdma(buf.at[rs, hs], buf.at[rs, hs], ag_ss.at[p, j, s, 0], ag_rs.at[p, j, s, 0], dev).wait_recv()
            go(rdma(buf.at[rs, hs], buf.at[rs, hs], fw_ss.at[p, j, s], fw_rs.at[p, j, s], dev))

    def gather_cross(p, buf, j):
        cs = pl.ds(j * width, width)
        for s, dev, blk_id in ((0, right, b_left), (1, left, b_right)):
            rs = pl.ds(own_cls + blk_id, blk)
            hs = pl.ds(j * width + (1 - s) * half, half)
            rdma(buf.at[rs, hs], buf.at[rs, hs], ag_ss.at[p, j, s, 1], ag_rs.at[p, j, s, 1], dev).wait_recv()
            go(rdma(buf.at[rs, cs], buf.at[rs, cs], d2d_ss.at[p, j, 1 + s], d2d_rs.at[p, j, 1 + s], other))

    def gather_far(p, buf, j):
        cs = pl.ds(j * width, width)
        rs = pl.ds(own_cls + b_far, blk)
        for s, dev in ((0, right), (1, left)):
            hs = pl.ds(j * width + s * half, half)
            rdma(buf.at[rs, hs], buf.at[rs, hs], fw_ss.at[p, j, s], fw_rs.at[p, j, s], dev).wait_recv()
        go(rdma(buf.at[rs, cs], buf.at[rs, cs], d2d_ss.at[p, j, 3], d2d_rs.at[p, j, 3], other))

    def gather_wait(p, buf, j):
        cs = pl.ds(j * width, width)
        for k, blk_id in enumerate((b_own, b_left, b_right, b_far)):
            rs = pl.ds(oth_cls + blk_id, blk)
            rdma(buf.at[rs, cs], buf.at[rs, cs], d2d_ss.at[p, j, k], d2d_rs.at[p, j, k], other).wait_recv()

    x_load.wait()

    def finish_u(j, total):
        cs = pl.ds(j * width, width)
        x_mid[:, cs] = (x_own[:, cs].astype(F32) + total.astype(BF16).astype(F32)).astype(BF16)

    reduce_scatter(0, lambda: z_ref[pl.ds(own_cls, cls_rows), :], lambda: z_ref[pl.ds(oth_cls, cls_rows), :], wo, 'o', finish_u)

    with jax.named_scope('ln2'):
        x1 = x_mid[...].astype(F32)
        mean = jnp.mean(x1, axis=-1, keepdims=True)
        centered = x1 - mean
        var = jnp.mean(centered * centered, axis=-1, keepdims=True)
        h_own = (centered * lax.rsqrt(var + NORM_EPS) * gain_ref[...] + bias_ref[...]).astype(BF16)
        h_all[pl.ds(own_cls + b_own, blk), :] = h_own
    gather_send(0, h_all, range(nc))
    for j in range(nc):
        loads['d', j].start()

    up = None
    for name, stage in (('gforward', gather_forward), ('gcross', gather_cross), ('gfar', gather_far)):
        for j in range(nc):
            with jax.named_scope(f'{name}0{j}'):
                stage(0, h_all, j)
    for j in range(nc):
        with jax.named_scope(f'gwait0{j}'):
            gather_wait(0, h_all, j)
        with jax.named_scope(f'up{j}'):
            loads['u', j].wait()
            cs = pl.ds(j * width, width)
            part = jnp.dot(h_all[:, cs], wu[cs, :], preferred_element_type=F32)
            up = part if up is None else up + part
    with jax.named_scope('gelu'):
        act[...] = (0.5 * up * (1.0 + lax.erf(up * (0.5 ** 0.5)))).astype(BF16)

    def finish_f(j, total):
        cs = pl.ds(j * width, width)
        x2 = x_mid[:, cs].astype(F32) + total.astype(BF16).astype(F32)
        out_ref[pl.ds(own_cls + b_own, blk), cs] = x2.astype(BF16)
        gather_send(1, out_ref, [j])

    reduce_scatter(1, lambda: act[pl.ds(own_cls, cls_rows), :], lambda: act[pl.ds(oth_cls, cls_rows), :], wd, 'd', finish_f)
    for name, stage in (('gforward', gather_forward), ('gcross', gather_cross), ('gfar', gather_far)):
        for j in range(nc):
            with jax.named_scope(f'{name}1{j}'):
                stage(1, out_ref, j)
    for j in range(nc):
        with jax.named_scope(f'gwait1{j}'):
            gather_wait(1, out_ref, j)
    with jax.named_scope('drain'):
        for copy in sends:
            copy.wait_send()


def tail(z, x2d, w_o, w_up, w_down, gain, bias):
    rows, d_model = x2d.shape
    inner = z.shape[1]
    ffn = w_up.shape[1]
    nc = NUM_CHUNKS
    blk = rows // 8
    dma = pltpu.SemaphoreType.DMA
    vmem = pl.BlockSpec(memory_space=pltpu.VMEM)
    hbm = pl.BlockSpec(memory_space=pl.ANY)
    return pl.pallas_call(
        tail_kernel,
        out_shape=jax.ShapeDtypeStruct((rows, d_model), BF16),
        in_specs=[vmem, hbm, hbm, hbm, hbm, vmem, vmem],
        out_specs=vmem,
        scratch_shapes=[
            pltpu.VMEM((inner, d_model), BF16),
            pltpu.VMEM((d_model, ffn), BF16),
            pltpu.VMEM((ffn, d_model), BF16),
            pltpu.VMEM((blk, d_model), BF16),
            pltpu.VMEM((rows // 2, d_model), F32),
            pltpu.VMEM((rows, ffn), BF16),
            pltpu.VMEM((rows, d_model), BF16),
            pltpu.VMEM((blk, d_model), BF16),
            pltpu.VMEM((2, rows // 2, d_model), BF16),
            pltpu.VMEM((2, rows // 2, d_model), BF16),
            pltpu.VMEM((2, blk, d_model), BF16),
            pltpu.VMEM((2, blk, d_model), BF16),
            pltpu.VMEM((2, 2, blk, d_model), BF16),
            pltpu.VMEM((2, 2, blk, d_model), BF16),
            dma((3, nc)),
            dma,
            dma((2, nc)), dma((2, nc)),
            dma((2, nc, 2)), dma((2, nc, 2)),
            dma((2, nc, 2, 2)), dma((2, nc, 2, 2)),
            dma((2, nc, 2, 2)), dma((2, nc, 2, 2)),
            dma((2, nc, 2)), dma((2, nc, 2)),
            dma((2, nc, 4)), dma((2, nc, 4)),
        ],
        compiler_params=pltpu.CompilerParams(collective_id=0, has_side_effects=True, vmem_limit_bytes=60 * 1024 * 1024),
        name='tail',
    )(z, x2d, w_o, w_up, w_down, gain, bias)


def solution(mesh):
    n_tp = mesh.shape['tp']

    def local_layer(x_in, start_pos, kv_state, ln1_gain, ln1_bias, w_q, w_k, w_v, w_g, w_o, ln2_gain, ln2_bias, w_up, w_down):
        batch, chunk_len, d_model = x_in.shape
        _, local_heads, key_dim, _ = kv_state.shape
        x2d = x_in.reshape(batch * chunk_len, d_model)
        log_gamma = np.log1p(-np.exp2(-5.0 - np.arange(local_heads * n_tp))).astype(np.float32)
        freq = np.power(ROPE_BASE, -np.arange(key_dim // 2) / (key_dim // 2)).astype(np.float32).reshape(1, -1)
        mixed, new_state = head(start_pos, jnp.asarray(log_gamma), jnp.asarray(freq), ln1_gain.reshape(1, -1), ln1_bias.reshape(1, -1),
                                x2d, kv_state, w_q, w_k, w_v, w_g)
        x_out = tail(mixed, x2d, w_o, w_up, w_down, ln2_gain.reshape(1, -1), ln2_bias.reshape(1, -1))
        return x_out.reshape(x_in.shape), new_state

    in_specs = (P('dp', None, None), P('dp'), P('dp', 'tp', None, None), P(), P(), P(None, 'tp'), P(None, 'tp'), P(None, 'tp'), P(None, 'tp'), P('tp', None), P(), P(), P(None, 'tp'), P('tp', None))
    out_specs = (P('dp', None, None), P('dp', 'tp', None, None))
    return jax.shard_map(local_layer, mesh=mesh, in_specs=in_specs, out_specs=out_specs, check_vma=False)
```

time: 89.1 us -> 62.5 us (0.70)
  matrix products: 17.3 us -> 0 us
  other arithmetic: 6.81 us -> 0 us
  local copies, waits for them, and re-layouts: 4.18 us -> 2.29 us
    dot_general x7 -> x0, matrix products: 17.3 us -> none  [the longest x1 5.55 us: project_heads(): jnp.einsum('bcd,dhe->bche', h_one, w_v.reshape(d_model, num_heads, val_di...]
    pallas_call x1, Pallas kernels: 59.8 us -> 47.1 us  [tail(): pl.pallas_call(tail_kernel, out_shape=jax.ShapeDtypeStruct((rows, d_model...]
    pallas_call x0 -> x1, Pallas kernels: none -> 12.2 us  [head(): pl.pallas_call(head_kernel, out_shape=(jax.ShapeDtypeStruct((rows, heads...]
    reduce_sum x3 -> x0, other arithmetic: 4.34 us -> none  [the longest x1 1.65 us: layer_norm(): variance = jnp.mean(centered * centered, axis=-1, keepdims=True)]
    unnamed x20 -> x1, local copies, waits for them, and re-layouts: 3.91 us -> 2.29 us
where the time goes in v2:
time: 62.5 us; the launch traced here: 62.3 us
  Pallas kernels  59.4 us (95%)
  local copies, waits for them, and re-layouts  2.29 us (4%)
  between operations  0.65 us (1%)
    pallas_call x1, Pallas kernels, tail(): pl.pallas_call(tail_kernel, out_shape=jax.ShapeDtypeStruct((rows, d_model...  47.1 us
    pallas_call x1, Pallas kernels, head(): pl.pallas_call(head_kernel, out_shape=(jax.ShapeDtypeStruct((rows, heads...  12.2 us
    unnamed x1, local copies, waits for them, and re-layouts  2.29 us

profile of v2, /device:TPU:81, one launch (start us, length us, event | category | flops | bytes accessed | tf_op | source)
XLA Modules:
  0.0 62.3 jit_solution(76914295687160591)
XLA Ops:
  0.6 12.2 %head.1 = (bf16[128,1024]{1,0:T(8,128)(2,1)}, f32[2,2,256,512]{3,2,1,0:T(8,128)}) custom-call(s32[2]{0:T(128)} %pos_ref.1, f32[16]{0:T(128)} %constant.4.clone.lg_ref, f32[1,128]{1,0:T(1,128)} %constant.5.clone.freq_ref, f32[1,4096]{1,0:T(1,128)} %bitcast.9, f32[1,4096]{1,0:T(1,128)} %bitcast.10, bf16[128,4096]{1,0:T(8,128)(2,1)} %bitcast.7, ...), custom_call_target="tpu_custom_call" | custom-call | tf_op jit(solution)/shard_map/head/pallas_call | solution.py:150
  12.9 47.1 %tail.1 = bf16[128,4096]{1,0:T(8,128)(2,1)} custom-call(bf16[128,1024]{1,0:T(8,128)(2,1)} %get-tuple-element.4.z_ref, bf16[128,4096]{1,0:T(8,128)(2,1)} %bitcast.8, bf16[1024,4096]{1,0:T(8,128)(2,1)} %wo_hbm.1, bf16[4096,1024]{1,0:T(8,128)(2,1)} %wu_hbm.1, bf16[1024,4096]{1,0:T(8,128)(2,1)} %wd_hbm.1, f32[1,4096]{1,0:T(1,128)} %bitcast.11, f32[1,4096]{1,0:T(1,128)} %bitcast.12), custom_call_target="tpu_custom_call" | custom-call | tf_op jit(solution)/shard_map/tail/pallas_call | solution.py:382
  60.0 2.3 %copy.19 = bf16[2,64,4096]{2,1,0:T(8,128)(2,1)} copy(bf16[2,64,4096]{2,1,0:T(8,128)(2,1)} %bitcast.6) | data formatting | bytes 2097152
